TPU v7x, 256 devices: a whole 4x4x8 slice. The times are simulated.
256 devices in a mesh: row: 32 (over z, x), col: 8 (over y, core).
Axes of the slice: x: 4, y: 4, z: 8, core: 2. Of those that a mesh axis runs over, the one named last changes fastest.
Arguments:
- integrals: bfloat16 [65536, 8192], P('row', 'col'), may hold values from -0.0234375 to 0.0234375
- lambda2: bfloat16 [2016, 65536], P('col', 'row'), may hold values from -6 to 6
- source_terms: float32 [2016, 8192], P('row', 'col'), may hold values from -6 to 6
- hist_amp: bfloat16 [5, 2016, 8192], P(None, 'row', 'col'), may hold values from -6 to 6
- hist_err: bfloat16 [5, 2016, 8192], P(None, 'row', 'col'), may hold values from -64 to 64
- eps_occ: float32 [64], replicated, may hold values from -1 to -0.3
- eps_vir: float32 [800], replicated, may hold values from 0.1 to 1
- occ_pair: int32 [2, 2016], P(None, 'row'), may hold values from 0 to 63, as said below
- vir_pair: int32 [2, 8192], P(None, 'col'), may hold values from 0 to 799, as said below
Outputs:
- updated: float32 [2016, 8192], P('row', 'col')
Inputs may be any that keep to these rules, and one draw needn't show every extreme that they name: `occ_pair`: every pair i < j of the 64 occupied orbitals appears exactly once, in some order. `vir_pair`: in every column the first orbital is smaller than the second.
All inputs are finite; a program needn't handle non-finite values.
Results may differ from a plain program's by a relative error of at most 0.0003.
Values may be sent and summed in bfloat16 or wider, within the bound.
A program may use at most 64 MiB of HBM per device.

v0:
```python
import jax
import jax.numpy as jnp
from jax import lax
from jax.sharding import PartitionSpec as P

precise = lax.Precision.HIGHEST


def pair_energy(pairs, energies):
    levels = jnp.arange(energies.shape[0], dtype=jnp.int32)
    first = jnp.sum(jnp.where(pairs[0][:, None] == levels[None, :], energies[None, :], 0.0), axis=1)
    second = jnp.sum(
        jnp.where(pairs[1][:, None] == levels[None, :], energies[None, :], 0.0), axis=1
    )
    return first + second


def diis_weights(correlation):
    factor = jnp.linalg.cholesky(correlation)
    order = correlation.shape[0]
    forward = []
    for k in range(order):
        running = jnp.ones((), correlation.dtype)
        for m in range(k):
            running = running - factor[k, m] * forward[m]
        forward.append(running / factor[k, k])
    backward = [None] * order
    for k in reversed(range(order)):
        running = forward[k]
        for m in range(k + 1, order):
            running = running - factor[m, k] * backward[m]
        backward[k] = running / factor[k, k]
    solved = jnp.stack(backward)
    return solved / jnp.sum(solved)


def on_device(
    integrals, lambda2, source_terms, hist_amp, hist_err, eps_occ, eps_vir, occ_pair, vir_pair
):
    stored_count = hist_err.shape[0]
    flat_stored = hist_err.astype(jnp.float32).reshape(stored_count, -1)
    all_cols = lax.all_gather(lambda2, "col", axis=0, tiled=True)
    ladder = lax.psum_scatter(
        jnp.dot(all_cols, integrals, preferred_element_type=jnp.float32),
        "row",
        scatter_dimension=0,
        tiled=True,
    )
    denominator = pair_energy(occ_pair, eps_occ)[:, None] - pair_energy(vir_pair, eps_vir)[None, :]
    raw_update = (source_terms + ladder) / denominator
    err_new = raw_update - hist_amp[0].astype(jnp.float32)
    flat_new = err_new.reshape(1, -1)
    stacked = jnp.concatenate([flat_stored, flat_new], axis=0)
    correlation = lax.psum(jnp.dot(stacked, stacked.T, precision=precise), ("row", "col"))
    weights = diis_weights(correlation)
    updated = weights[stored_count] * raw_update
    for k in range(stored_count):
        updated = updated + weights[k] * hist_amp[k].astype(jnp.float32)
    return updated


def solution(mesh):
    placed = (
        P("row", "col"),
        P("col", "row"),
        P("row", "col"),
        P(None, "row", "col"),
        P(None, "row", "col"),
        P(),
        P(),
        P(None, "row"),
        P(None, "col"),
    )
    return jax.shard_map(
        on_device, mesh=mesh, in_specs=placed, out_specs=P("row", "col"), check_vma=False
    )
```

profile of v0, /device:TPU:1, one launch (start us, length us, event | category | flops | bytes accessed | tf_op | source)
XLA Modules:
  0.0 320.9 jit_solution(15406420744793112163)
XLA Ops:
  6.5 0.7 all-gather.3.cloned.1.call-update
  7.3 0.8 fusion.14
  8.0 1.5 select_reduce_fusion
  9.6 1.2 convert_bitcast_fusion
  10.8 54.8 %all-gather.3.cloned.1.call-done = bf16[8,252,2048]{2,1,0:T(8,128)(2,1)} async-done(((bf16[1,252,2048]{2,1,0:T(8,128)(2,1)}), bf16[8,252,2048]{2,1,0:T(8,128)(2,1)}) %all-gather.3.cloned.1.call-update) | async-done | bytes 8257552 | tf_op jit(solution)/shard_map/all_gather | solution.py:42
  65.7 7.5 %reshape.68 = bf16[2016,2048]{1,0:T(8,128)(2,1)} reshape(bf16[8,252,2048]{2,1,0:T(8,128)(2,1)} %all-gather.3.cloned.1.call-done) | data formatting | bytes 16515072
  73.1 14.2 %fusion.18 = f32[2016,1024]{1,0:T(8,128)} fusion(bf16[2016,2048]{1,0:T(8,128)(2,1)} %reshape.68, bf16[2048,1024]{1,0:T(8,128)(2,1)} %param.9), kind=kOutput, calls=%fused_computation.38 | convolution fusion | flops 8455716864 | bytes 20709376 | tf_op jit(solution)/shard_map/dot_general | solution.py:44
  87.4 100.2 %fusion = f32[64,1024]{1,0:T(8,128)S(1)} fusion(f32[2016,1024]{1,0:T(8,128)} %fusion.18), kind=kCustom, calls=%all-reduce-scatter | all-reduce-scatter fusion | flops 2097153 | bytes 8520704
  187.6 0.0 copy-start
  187.6 0.0 copy-start.5
  187.6 0.0 copy-start.4
  187.6 2.3 collective-permute-start
  190.0 0.8 copy.19
  190.8 0.0 copy-start.1
  190.8 0.0 copy-start.2
  190.8 0.6 dynamic-slice.4
  192.0 0.2 select_reduce_fusion.2
  192.2 0.0 collective-permute-done
  192.2 2.0 concatenate.4
  194.2 1.1 fusion.5
  195.3 0.3 copy.20
  195.6 4.5 %fusion.1 = f32[6,6]{0,1:T(8,128)S(1)} fusion(f32[1,64512]{1,0:T(1,128)S(1)} %bitcast.70, f32[5,64512]{1,0:T(8,128)S(1)} %bitcast.68), kind=kOutput, calls=%fused_computation.4 | convolution fusion | flops 28256256 | bytes 1548432 | tf_op jit(solution)/shard_map/dot_general | solution.py:54
  200.1 78.7 %psum.7 = f32[6,6]{0,1:T(8,128)S(1)} all-reduce(f32[6,6]{0,1:T(8,128)S(1)} %fusion.1), channel_id=1, replica_groups=mesh['row'=32,'col'=8] {'row','col'}, use_global_device_ids=true, to_apply=%region_5.6 | all-reduce | flops 36 | bytes 288 | tf_op jit(solution)/shard_map/psum | solution.py:54
  278.8 0.1 copy.17
  278.9 0.5 cholesky.18
  279.4 0.6 compare_reduce_fusion
  280.1 0.6 select_select_fusion
  280.7 0.6 fusion.16
  281.3 0.7 fusion.15
  308.7 0.1 stack.27
  308.7 0.7 fusion.17
  309.4 4.6 %fusion.10 = f32[63,1024]{1,0:T(8,128)} fusion(bf16[5,63,1024]{2,1,0:T(8,128)(2,1)S(1)} %copy-done.2, f32[]{:T(128)} %bitcast.43, f32[]{:T(128)} %bitcast.41, f32[]{:T(128)} %bitcast.39, f32[]{:T(128)} %bitcast.37, f32[]{:T(128)} %bitcast.35, f32[]{:T(128)} %bitcast.34, f32[1024]{0:T(1024)S(1)} %add.47, f32[63]{0:T(128)S(1)} %add.46, ...), kind=kLoop, calls=%fused_computation.16 | loop fusion | flops 1225728 | bytes 1423640 | tf_op jit(solution)/shard_map/add | solution.py:58
  (15 shorter events, 0.1 us)
Async XLA Ops:
  6.5 59.1 %all-gather.3.cloned.1.call-start = ((), (), s32[]{:S(2)}) async-start(), calls=%async_computation | async-start | bytes 9437184 | tf_op jit(solution)/shard_map/all_gather | solution.py:42
  87.4 102.6 %copy-start.3 = (s32[2,63]{1,0:T(2,128)S(1)}, s32[2,63]{1,0:T(2,128)}, u32[]{:S(2)}) copy-start(s32[2,63]{1,0:T(2,128)} %param.16) | copy-start | bytes 1516
  187.6 2.4 copy-start
  187.6 3.2 copy-start.5
  187.6 4.3 %copy-start.4 = (f32[64]{0:T(128)S(1)}, f32[64]{0:T(128)}, u32[]{:S(2)}) copy-start(f32[64]{0:T(128)} %param.14) | copy-start | bytes 772
  187.6 4.5 %collective-permute-start = (f32[31,1024]{1,0:T(8,128)S(1)}, f32[31,1024]{1,0:T(8,128)}, u32[]{:S(2)}, u32[]{:S(2)}) collective-permute-start(f32[31,1024]{1,0:T(8,128)S(1)} %slice.172), channel_id=1, source_target_pairs={{0,8},{8,16},{16,24},{24,32},{32,40},{40,48},{48,56},{56,64},{64,7... | collective-permute-start | bytes 380936
  190.8 118.6 %copy-start.1 = (f32[63,1024]{1,0:T(8,128)S(1)}, f32[63,1024]{1,0:T(8,128)}, u32[]{:S(2)}) copy-start(f32[63,1024]{1,0:T(8,128)} %param.11) | copy-start | bytes 774148
  190.8 118.6 %copy-start.2 = (bf16[5,63,1024]{2,1,0:T(8,128)(2,1)S(1)}, bf16[5,63,1024]{2,1,0:T(8,128)(2,1)}, u32[]{:S(2)}) copy-start(bf16[5,63,1024]{2,1,0:T(8,128)(2,1)} %param.12) | copy-start | bytes 1935364
Sparse Core Ops, SparseCore 0:
  9.2 56.4 all-gather.2
where the time goes:
time: 322 us; the launch traced here: 321 us
  blocking collectives  179 us (56%)
  waiting for transfers between devices  55.6 us (17%)
  between operations  40.7 us (13%)
  matrix products  18.7 us (6%)
  local copies, waits for them, and re-layouts  14.1 us (4%)
  other arithmetic  10.6 us (3%)
    unnamed x1, blocking collectives  100 us
    psum x1, blocking collectives, on_device(): lax.psum(jnp.dot(stacked, stacked.T, precision=precise), ('row', 'col'))  78.7 us
    all_gather x1, waiting for transfers between devices, on_device(): all_cols = lax.all_gather(lambda2, 'col', axis=0, tiled=True)  54.8 us
    dot_general x1, matrix products, on_device(): jnp.dot(all_cols, integrals, preferred_element_type=jnp.float32)  14.2 us
    unnamed x18, local copies, waits for them, and re-layouts  11.2 us
  transfers between devices with their start and end apart: 2, of which 1 were waited for; matrix products, arithmetic and copies ran while one was open for 2% of the time, Pallas kernels for 0%

commit v1 on v0

--- a/solution.py
+++ b/solution.py
@@ -39,7 +39,9 @@
 ):
     stored_count = hist_err.shape[0]
     flat_stored = hist_err.astype(jnp.float32).reshape(stored_count, -1)
-    all_cols = lax.all_gather(lambda2, "col", axis=0, tiled=True)
+    all_cols = jnp.concatenate(
+        lax.all_to_all(jnp.stack([lambda2] * lax.axis_size("col")), "col", 0, 0), axis=0
+    )
     ladder = lax.psum_scatter(
         jnp.dot(all_cols, integrals, preferred_element_type=jnp.float32),
         "row",

time: 322 us -> 357 us (1.11)
  waiting for transfers between devices: 55.6 us -> 92.8 us
  between operations: 40.7 us -> 27.3 us
  starting transfers between devices: 2.31 us -> 11 us
  local copies, waits for them, and re-layouts: 14.1 us -> 18.9 us
    all_to_all x0 -> x1, waiting for transfers between devices: none -> 92.8 us  [on_device(): lax.all_to_all(jnp.stack([lambda2] * lax.axis_size('col')), 'col', 0, 0)]
    all_gather x1 -> x0, waiting for transfers between devices: 54.8 us -> none  [on_device(): all_cols = lax.all_gather(lambda2, 'col', axis=0, tiled=True)]
    all_to_all x0 -> x1, starting transfers between devices: none -> 8.17 us  [on_device(): lax.all_to_all(jnp.stack([lambda2] * lax.axis_size('col')), 'col', 0, 0)]
    reshape x0 -> x1, local copies, waits for them, and re-layouts: none -> 7.46 us  [on_device(): jnp.concatenate(lax.all_to_all(jnp.stack([lambda2] * lax.axis_size('col')...]
    unnamed x18 -> x23, local copies, waits for them, and re-layouts: 11.2 us -> 3.7 us
    another operation x0 -> x1, local copies, waits for them, and re-layouts: none -> 5.51 us  [on_device(): jnp.stack([lambda2] * lax.axis_size('col'))]
  transfers between devices with their start and end apart: 2 -> 2, of which waited for: 1 -> 1; matrix products, arithmetic and copies ran while one was open for 2% -> 1% of each run, Pallas kernels for 0% -> 0%
where the time goes in v1:
time: 357 us; the launch traced here: 356 us
  blocking collectives  178 us (50%)
  waiting for transfers between devices  92.8 us (26%)
  between operations  27.3 us (8%)
  local copies, waits for them, and re-layouts  18.9 us (5%)
  matrix products  18.7 us (5%)
  starting transfers between devices  11 us (3%)
  other arithmetic  8.77 us (2%)
    unnamed x1, blocking collectives  99.2 us
    all_to_all x1, waiting for transfers between devices, on_device(): lax.all_to_all(jnp.stack([lambda2] * lax.axis_size('col')), 'col', 0, 0)  92.8 us
    psum x1, blocking collectives, on_device(): lax.psum(jnp.dot(stacked, stacked.T, precision=precise), ('row', 'col'))  79.2 us
    dot_general x1, matrix products, on_device(): jnp.dot(all_cols, integrals, preferred_element_type=jnp.float32)  14.2 us
    all_to_all x1, starting transfers between devices, on_device(): lax.all_to_all(jnp.stack([lambda2] * lax.axis_size('col')), 'col', 0, 0)  8.17 us
    reshape x1, local copies, waits for them, and re-layouts, on_device(): jnp.concatenate(lax.all_to_all(jnp.stack([lambda2] * lax.axis_size('col')...  7.46 us
  transfers between devices with their start and end apart: 2, of which 1 were waited for; matrix products, arithmetic and copies ran while one was open for 1% of the time, Pallas kernels for 0%

profile of v1, /device:TPU:1, one launch (start us, length us, event | category | flops | bytes accessed | tf_op | source)
XLA Modules:
  0.0 355.9 jit_solution(6870656481076839429)
XLA Ops:
  0.0 5.5 %stack.32 = bf16[8,252,2048]{2,1,0:T(8,128)(2,1)} broadcast(bf16[252,2048]{1,0:T(8,128)(2,1)} %param.10), dimensions={1,2} | broadcast | bytes 9289728 | tf_op jit(solution)/shard_map/stack | solution.py:43
  5.5 8.2 %all-to-all-start = ((bf16[8,252,2048]{2,1,0:T(8,128)(2,1)}), bf16[8,252,2048]{2,1,0:T(8,128)(2,1)}, u32[]{:S(2)}, u32[]{:S(2)}) async-start(bf16[8,252,2048]{2,1,0:T(8,128)(2,1)} %stack.32), calls=%async_computation | async-start | bytes 16777216 | tf_op jit(solution)/shard_map/all_to_all | solution.py:43
  13.7 0.8 select_reduce_fusion
  14.5 0.1 convert_bitcast_fusion
  14.6 92.8 %all-to-all-done = bf16[8,252,2048]{2,1,0:T(8,128)(2,1)} async-done(((bf16[8,252,2048]{2,1,0:T(8,128)(2,1)}), bf16[8,252,2048]{2,1,0:T(8,128)(2,1)}, u32[]{:S(2)}, u32[]{:S(2)}) %all-to-all-start) | async-done | bytes 8257568 | tf_op jit(solution)/shard_map/all_to_all | solution.py:43
  107.4 7.5 %reshape.67 = bf16[2016,2048]{1,0:T(8,128)(2,1)} reshape(bf16[8,252,2048]{2,1,0:T(8,128)(2,1)} %all-to-all-done) | data formatting | bytes 16515072 | tf_op jit(solution)/shard_map/reshape | solution.py:42
  114.9 14.2 %fusion.18 = f32[2016,1024]{1,0:T(8,128)} fusion(bf16[2016,2048]{1,0:T(8,128)(2,1)} %reshape.67, bf16[2048,1024]{1,0:T(8,128)(2,1)} %param.9), kind=kOutput, calls=%fused_computation.38 | convolution fusion | flops 8455716864 | bytes 20709376 | tf_op jit(solution)/shard_map/dot_general | solution.py:46
  129.1 99.2 %fusion = f32[64,1024]{1,0:T(8,128)S(1)} fusion(f32[2016,1024]{1,0:T(8,128)} %fusion.18), kind=kCustom, calls=%all-reduce-scatter | all-reduce-scatter fusion | flops 2097153 | bytes 8520704
  228.3 0.0 copy-start
  228.3 0.0 copy-start.7
  228.3 0.0 copy-start.8
  228.4 2.8 collective-permute-start
  231.2 0.8 copy.19
  232.0 0.0 copy-start.1
  232.0 0.0 copy-start.2
  232.0 0.2 select_reduce_fusion.2
  232.3 0.6 dynamic-slice.4
  233.4 0.0 collective-permute-done
  233.4 2.0 concatenate.4
  235.4 1.1 fusion.5
  236.6 0.3 copy.20
  236.8 4.5 %fusion.1 = f32[6,6]{0,1:T(8,128)S(1)} fusion(f32[1,64512]{1,0:T(1,128)S(1)} %bitcast.68, f32[5,64512]{1,0:T(8,128)S(1)} %bitcast.67), kind=kOutput, calls=%fused_computation.4 | convolution fusion | flops 28256256 | bytes 1548432 | tf_op jit(solution)/shard_map/dot_general | solution.py:56
  241.3 79.2 %psum.7 = f32[6,6]{0,1:T(8,128)S(1)} all-reduce(f32[6,6]{0,1:T(8,128)S(1)} %fusion.1), channel_id=1, replica_groups=mesh['row'=32,'col'=8] {'row','col'}, use_global_device_ids=true, to_apply=%region_5.6 | all-reduce | flops 36 | bytes 288 | tf_op jit(solution)/shard_map/psum | solution.py:56
  320.6 0.1 copy.17
  320.7 0.5 cholesky.18
  321.2 0.6 compare_reduce_fusion
  321.9 0.6 select_select_fusion
  322.5 0.6 fusion.16
  323.1 0.7 fusion.15
  350.4 0.1 stack.39
  350.5 0.7 fusion.17
  351.2 4.6 %fusion.10 = f32[63,1024]{1,0:T(8,128)} fusion(bf16[5,63,1024]{2,1,0:T(8,128)(2,1)S(1)} %copy-done.2, f32[]{:T(128)} %bitcast.42, f32[]{:T(128)} %bitcast.40, f32[]{:T(128)} %bitcast.38, f32[]{:T(128)} %bitcast.36, f32[]{:T(128)} %bitcast.34, f32[]{:T(128)} %bitcast.33, f32[1024]{0:T(1024)S(1)} %add.47, f32[63]{0:T(128)S(1)} %add.46, ...), kind=kLoop, calls=%fused_computation.16 | loop fusion | flops 1225728 | bytes 1423640 | tf_op jit(solution)/shard_map/add | solution.py:60
  (21 shorter events, 0.1 us)
Async XLA Ops:
  5.5 8.2 %copy-start.4 = (s32[2,1024]{1,0:T(2,128)S(1)}, s32[2,1024]{1,0:T(2,128)}, u32[]{:S(2)}) copy-start(s32[2,1024]{1,0:T(2,128)} %param.17) | copy-start | bytes 24580
  5.5 8.2 %copy-start.5 = (f32[800]{0:T(1024)S(1)}, f32[800]{0:T(1024)}, u32[]{:S(2)}) copy-start(f32[800]{0:T(1024)} %param.15) | copy-start | bytes 9604
  5.5 9.0 %copy-start.3 = (bf16[5,63,1024]{2,1,0:T(8,128)(2,1)S(1)}, bf16[5,63,1024]{2,1,0:T(8,128)(2,1)}, u32[]{:S(2)}) copy-start(bf16[5,63,1024]{2,1,0:T(8,128)(2,1)} %param.13) | copy-start | bytes 1935364
  5.5 101.9 %all-to-all-start = ((bf16[8,252,2048]{2,1,0:T(8,128)(2,1)}), bf16[8,252,2048]{2,1,0:T(8,128)(2,1)}, u32[]{:S(2)}, u32[]{:S(2)}) async-start(bf16[8,252,2048]{2,1,0:T(8,128)(2,1)} %stack.32), calls=%async_computation | async-start | bytes 16777216 | tf_op jit(solution)/shard_map/all_to_all | solution.py:43
  129.1 102.0 %copy-start.6 = (s32[2,63]{1,0:T(2,128)S(1)}, s32[2,63]{1,0:T(2,128)}, u32[]{:S(2)}) copy-start(s32[2,63]{1,0:T(2,128)} %param.16) | copy-start | bytes 1516
  228.3 2.9 copy-start
  228.3 3.7 %copy-start.7 = (f32[64]{0:T(128)S(1)}, f32[64]{0:T(128)}, u32[]{:S(2)}) copy-start(f32[64]{0:T(128)} %param.14) | copy-start | bytes 772
  228.3 3.9 %copy-start.8 = (u32[256]{0:T(256)S(1)}, u32[256]{0:T(256)}, u32[]{:S(2)}) copy-start(u32[256]{0:T(256)} %constant.47) | copy-start | bytes 3076
  228.4 5.0 %collective-permute-start = (f32[31,1024]{1,0:T(8,128)S(1)}, f32[31,1024]{1,0:T(8,128)}, u32[]{:S(2)}, u32[]{:S(2)}) collective-permute-start(f32[31,1024]{1,0:T(8,128)S(1)} %slice.172), channel_id=1, source_target_pairs={{0,8},{8,16},{16,24},{24,32},{32,40},{40,48},{48,56},{56,64},{64,7... | collective-permute-start | bytes 380936
  232.0 119.2 %copy-start.1 = (f32[63,1024]{1,0:T(8,128)S(1)}, f32[63,1024]{1,0:T(8,128)}, u32[]{:S(2)}) copy-start(f32[63,1024]{1,0:T(8,128)} %param.11) | copy-start | bytes 774148
  232.0 119.2 %copy-start.2 = (bf16[5,63,1024]{2,1,0:T(8,128)(2,1)S(1)}, bf16[5,63,1024]{2,1,0:T(8,128)(2,1)}, u32[]{:S(2)}) copy-start(bf16[5,63,1024]{2,1,0:T(8,128)(2,1)} %param.12) | copy-start | bytes 1935364
